TPU v7x, 32 devices: a whole 2x2x4 slice. The times are simulated.
32 devices in a mesh: dp: 4 (over z), tp: 8 (over y, x, core).
Axes of the slice: x: 2, y: 2, z: 4, core: 2. Of those that a mesh axis runs over, the one named last changes fastest.
Arguments:
- hidden: bfloat16 [16, 1024, 1024], P('dp')
- labels: int32 [16, 1024], P('dp')
- loss_mask: int32 [16, 1024], P('dp')
- norm_gain: bfloat16 [1024], replicated
- w_out: bfloat16 [1024, 50304], P(None, 'tp')
Outputs:
- output 1: float32 [], replicated
- output 2: bfloat16 [16, 1024, 1024], P('dp')
- output 3: float32 [1024], replicated
- output 4: float32 [1024, 50304], P(None, 'tp')
All inputs are finite; a program needn't handle non-finite values.
Results may differ from a plain program's by a relative error of at most 0.001.
Values sent between devices are 32-bit elements.
A program may use at most 1 GiB of HBM per device.

v0:
```python
import jax
import jax.numpy as jnp
from jax import lax
from jax.sharding import PartitionSpec as P

EPS_NORM = 1e-5


def solution(mesh):
    def local_step(hidden, labels, loss_mask, norm_gain, w_shard):
        n_rows, seq_len, model_dim = hidden.shape
        shard_vocab = w_shard.shape[1]
        n_tokens = n_rows * seq_len
        x_tok = hidden.reshape(n_tokens, model_dim).astype(jnp.float32)
        inv_rms = lax.rsqrt(jnp.mean(x_tok * x_tok, axis=1, keepdims=True) + EPS_NORM)
        x_hat = x_tok * inv_rms
        gain_f = norm_gain.astype(jnp.float32)
        u_tok = (x_hat * gain_f).astype(jnp.bfloat16)
        logits = jnp.dot(u_tok, w_shard, preferred_element_type=jnp.float32)
        glob_max = lax.pmax(jnp.max(logits, axis=1, keepdims=True), "tp")
        shifted = jnp.exp(logits - glob_max)
        local_label = labels.reshape(n_tokens, 1) - lax.axis_index("tp") * shard_vocab
        is_label = lax.broadcasted_iota(jnp.int32, (1, shard_vocab), 1) == local_label
        part_stats = jnp.concatenate([jnp.sum(shifted, axis=1, keepdims=True), jnp.sum(jnp.where(is_label, logits, 0.0), axis=1, keepdims=True)], axis=1)
        full_stats = lax.psum(part_stats, "tp")
        sum_exp = full_stats[:, :1]
        log_norm = glob_max + jnp.log(sum_exp)
        target = full_stats[:, 1:]
        mask_f = loss_mask.reshape(n_tokens, 1).astype(jnp.float32)
        totals = lax.psum(jnp.stack([jnp.sum(mask_f), jnp.sum(mask_f * (log_norm - target))]), "dp")
        mask_count = totals[0]
        mean_loss = totals[1] / mask_count
        prob_tok = shifted / sum_exp
        d_logits = (jnp.where(is_label, prob_tok - 1.0, prob_tok) * (mask_f / mask_count)).astype(jnp.bfloat16)
        du_part = lax.dot_general(d_logits, w_shard, (((1,), (1,)), ((), ())), preferred_element_type=jnp.float32)
        du_tok = lax.psum(du_part, "tp")
        dw_part = lax.dot_general(u_tok, d_logits, (((0,), (0,)), ((), ())), preferred_element_type=jnp.float32)
        d_w_out = lax.psum(dw_part, "dp")
        d_gain = lax.psum(jnp.sum(du_tok * x_hat, axis=0), "dp")
        value_a6 = du_tok * gain_f
        dx_tok = inv_rms * (value_a6 - x_hat * jnp.mean(value_a6 * x_hat, axis=1, keepdims=True))
        d_hidden = dx_tok.astype(jnp.bfloat16).reshape(n_rows, seq_len, model_dim)
        return mean_loss, d_hidden, d_gain, d_w_out

    return jax.shard_map(local_step, mesh=mesh, in_specs=(P("dp", None, None), P("dp", None), P("dp", None), P(None), P(None, "tp")), out_specs=(P(), P("dp", None, None), P(None), P(None, "tp")), check_vma=False)
```

profile of v0, /device:TPU:0, one launch (start us, length us, event | category | flops | bytes accessed | tf_op | source)
XLA Modules:
  0.0 1392.6 jit_solution(14636103556842537062)
XLA Ops:
  7.2 0.0 all-reduce.3.cloned.1.call-start
  7.2 1.4 convert_reduce_fusion
  8.6 0.7 convert_bitcast_fusion
  9.3 0.7 convert_element_type.45
  10.0 0.7 subtract_bitcast_fusion
  10.7 0.6 copy.17
  11.3 0.6 copy.9
  11.9 5.1 multiply_reduce_fusion.2
  17.1 0.6 copy-done
  17.7 7.8 multiply_convert_fusion.1
  25.5 65.0 %fusion.7 = (f32[4096]{0:T(1024)S(1)}, f32[4096,6288]{0,1:T(8,128)}) fusion(bf16[4096,1024]{1,0:T(8,128)(2,1)} %multiply_convert_fusion.1, bf16[1024,6288]{0,1:T(8,128)(2,1)} %param.9), kind=kOutput, calls=%fused_computation.29 | convolution fusion | flops 52773318656 | bytes 124305408 | tf_op jit(solution)/shard_map/dot_general | solution.py:19
  90.5 25.6 %pmax.7 = f32[4096,1]{0,1:T(1,128)S(1)} all-reduce(f32[4096,1]{0,1:T(1,128)S(1)} %bitcast.59), channel_id=1, replica_groups=mesh['dp'=4,'tp'=8] {'tp'}, use_global_device_ids=true, to_apply=%region_3.0 | all-reduce | flops 4096 | bytes 32768 | tf_op jit(solution)/shard_map/pmax | solution.py:20
  116.0 32.2 %fusion.2 = (f32[4096]{0:T(1024)S(1)}, f32[4096]{0:T(1024)S(1)}) fusion(f32[4096,6288]{0,1:T(8,128)} %get-tuple-element.13, f32[4096]{0:T(1024)S(1)} %bitcast.50, s32[4096]{0:T(1024)S(1)} %bitcast.52), kind=kLoop, calls=%fused_computation.6 | loop fusion | flops 128770048 | bytes 103088128 | tf_op jit(solution)/shard_map/reduce_sum | solution.py:24
  148.3 22.4 %psum.35 = f32[4096,2]{0,1:T(2,128)S(1)} all-reduce(f32[4096,2]{0,1:T(2,128)S(1)} %pad_maximum_fusion), channel_id=1, replica_groups=mesh['dp'=4,'tp'=8] {'tp'}, use_global_device_ids=true, to_apply=%region_6.7 | all-reduce | flops 8192 | bytes 65536 | tf_op jit(solution)/shard_map/psum | solution.py:25
  170.6 0.0 copy-done.4
  170.6 0.6 fusion.5
  171.3 1.4 pad_maximum_fusion.1
  172.6 12.1 psum.36
  184.8 0.6 fusion.6
  185.4 0.7 divide_bitcast_fusion
  186.0 50.7 %fusion.1 = bf16[4096,6288]{0,1:T(8,128)(2,1)} fusion(f32[4096,6288]{0,1:T(8,128)} %get-tuple-element.13, f32[4096]{0:T(1024)S(1)} %bitcast.55, f32[4096]{0:T(1024)S(1)} %bitcast.54, s32[4096]{0:T(1024)S(1)} %bitcast.53, f32[4096]{0:T(1024)S(1)} %bitcast.51), kind=kLoop, calls=%fused_computation.2 | loop fusion | flops 180289536 | bytes 154599424 | tf_op jit(solution)/shard_map/convert_element_type | solution.py:34
  236.7 63.4 %fusion.8 = f32[4096,1024]{1,0:T(8,128)} fusion(bf16[4096,6288]{0,1:T(8,128)(2,1)} %fusion.1, bf16[1024,6288]{0,1:T(8,128)(2,1)} %param.9), kind=kOutput, calls=%fused_computation.30 | convolution fusion | flops 52747567104 | bytes 81166336 | tf_op jit(solution)/shard_map/dot_general | solution.py:35
  300.1 0.0 all-reduce.3.cloned.1.call-update
  300.2 0.0 all-reduce.5.cloned.1.call-start
  300.2 62.7 %fusion.9 = f32[1024,6288]{0,1:T(8,128)} fusion(bf16[4096,6288]{0,1:T(8,128)(2,1)} %fusion.1, bf16[4096,1024]{1,0:T(8,128)(2,1)} %multiply_convert_fusion.1), kind=kOutput, calls=%fused_computation.31 | convolution fusion | flops 52747567104 | bytes 85655552 | tf_op jit(solution)/shard_map/dot_general | solution.py:37
  362.9 0.0 all-reduce.5.cloned.1.call-update
  364.2 149.8 %all-reduce.3.cloned.1.call-done = f32[4096,1024]{1,0:T(8,128)} async-done(((f32[4096,1024]{1,0:T(8,128)}), f32[4096,1024]{1,0:T(8,128)}) %all-reduce.3.cloned.1.call-update) | async-done | bytes 16777232 | tf_op jit(solution)/shard_map/psum | solution.py:36
  513.9 10.0 multiply_reduce_fusion
  523.9 13.1 psum.38
  537.0 12.3 multiply_convert_fusion
  549.3 817.3 %all-reduce.5.cloned.1.call-done = f32[1024,6288]{0,1:T(8,128)} async-done(((f32[1024,6288]{0,1:T(8,128)}), f32[1024,6288]{0,1:T(8,128)}) %all-reduce.5.cloned.1.call-update) | async-done | bytes 25755664 | tf_op jit(solution)/shard_map/psum | solution.py:38
  1366.5 18.1 %copy.21 = f32[1024,6288]{0,1:T(8,128)} copy(f32[1024,6288]{0,1:T(8,128)} %all-reduce.5.cloned.1.call-done) | data formatting | bytes 51511296
  (17 shorter events, 0.1 us)
Async XLA Ops:
  7.2 506.8 %all-reduce.3.cloned.1.call-start = ((), (), s32[]{:S(2)}) async-start(), calls=%async_computation | async-start | bytes 33554432 | tf_op jit(solution)/shard_map/psum | solution.py:36
  10.0 80.5 %copy-start.5 = (f32[1024]{0:T(1024)}, f32[1024]{0:T(1024)S(1)}, u32[]{:S(2)}) copy-start(f32[1024]{0:T(1024)S(1)} %convert_element_type.45) | copy-start | bytes 12292
  17.1 0.6 copy-start
  25.5 90.5 %copy-start.3 = (s32[1,8,4,128]{3,1,2,0:T(8,128)S(1)}, s32[1,8,4,128]{3,1,2,0:T(8,128)}, u32[]{:S(2)}) copy-start(s32[1,8,4,128]{3,1,2,0:T(8,128)} %copy.17) | copy-start | bytes 49156
  116.0 54.6 %copy-start.4 = (f32[1,1,4,1024]{3,1,2,0:T(1,128)S(1)}, f32[1,1,4,1024]{3,1,2,0:T(1,128)}, u32[]{:S(2)}) copy-start(f32[1,1,4,1024]{3,1,2,0:T(1,128)} %copy.9) | copy-start | bytes 49156
  116.0 69.3 %copy-start.2 = (s32[4,1024]{1,0:T(4,128)S(1)}, s32[4,1024]{1,0:T(4,128)}, u32[]{:S(2)}) copy-start(s32[4,1024]{1,0:T(4,128)} %param.7) | copy-start | bytes 49156
  300.2 1066.4 %all-reduce.5.cloned.1.call-start = ((), (), s32[]{:S(2)}) async-start(), calls=%async_computation.1 | async-start | bytes 51511296 | tf_op jit(solution)/shard_map/psum | solution.py:38
  362.9 151.1 %copy-start.1 = (f32[1,8,4,128]{3,1,2,0:T(8,128)S(1)}, f32[1,8,4,128]{3,1,2,0:T(8,128)}, u32[]{:S(2)}) copy-start(f32[1,8,4,128]{3,1,2,0:T(8,128)} %copy-done) | copy-start | bytes 49156
  362.9 151.1 %copy-start.6 = (f32[1024]{0:T(1024)S(1)}, f32[1024]{0:T(1024)}, u32[]{:S(2)}) copy-start(f32[1024]{0:T(1024)} %copy-done.5) | copy-start | bytes 12292
Sparse Core Ops, SparseCore 0:
  300.3 213.6 all-reduce.2
  517.0 849.4 all-reduce.4
where the time goes:
time: 1390 us
  waiting for transfers between devices  967 us (70%)
  matrix products  191 us (14%)
  other arithmetic  124 us (9%)
  blocking collectives  73.1 us (5%)
  local copies, waits for them, and re-layouts  20.5 us (1%)
  between operations  16.5 us (1%)
    psum x1, waiting for transfers between devices, local_step(): d_w_out = lax.psum(dw_part, 'dp')  817 us
    psum x1, waiting for transfers between devices, local_step(): du_tok = lax.psum(du_part, 'tp')  150 us
    dot_general x1, matrix products, local_step(): logits = jnp.dot(u_tok, w_shard, preferred_element_type=jnp.float32)  65 us
    dot_general x1, matrix products, local_step(): lax.dot_general(d_logits, w_shard, (((1,), (1,)), ((), ())), preferred_el...  63.4 us
    dot_general x1, matrix products, local_step(): lax.dot_general(u_tok, d_logits, (((0,), (0,)), ((), ())), preferred_elem...  62.7 us
    convert_element_type x1, other arithmetic, local_step(): (jnp.where(is_label, prob_tok - 1.0, prob_tok) * (mask_f / mask_count)).a...  50.7 us
    reduce_sum x1, other arithmetic, local_step(): jnp.sum(shifted, axis=1, keepdims=True)  32.2 us
  transfers between devices with their start and end apart: 2, of which 2 were waited for; matrix products, arithmetic and copies ran while one was open for 6% of the time, Pallas kernels for 0%

commit v1 on v0

v1 whole, which is shorter than its diff:
```python
import functools

import jax
import jax.numpy as jnp
from jax import lax
from jax.experimental import pallas as pl
from jax.experimental.pallas import tpu as pltpu
from jax.sharding import PartitionSpec as P

EPS_NORM = 1e-5
LOG2E = 1.4426950408889634
F32 = jnp.float32
BF16 = jnp.bfloat16
ANY = pl.ANY
NT = (((1,), (1,)), ((), ()))
TN = (((0,), (0,)), ((), ()))


class Sizes:
    def __init__(self, tokens, width, vocab, pv, own, oc, osub, ac, asub, st):
        self.T, self.D, self.V = tokens, width, vocab
        self.PV, self.ST = pv, st
        self.OW, self.OC, self.OS = own, oc, osub
        self.RA, self.AC, self.AS = vocab - 2 * own, ac, asub
        self.PT = tokens // 4
        self.SL = tokens // 8
        self.SK = self.SL // 2
        self.NPV = vocab // pv
        self.RV = vocab - self.NPV * pv
        self.SG = tokens // 32
        self.AG = (asub + 15) // 16 * 8
        self.NOS, self.NAS = own // osub, self.RA // asub


def _kernel(z_, h, lab, msk, gain, wT, dw, dh, dg, loss, zh, unf, rb, rc, dub0, dub1, dub2,
            uv, unv, pb, zr, wr, da, da2, stg, hst, dhs, m8, s8, t8, lab8, lsev, mnv, mskn, labn, sts, strv, cntb, cntr, lsb, lsr, dgb, dgr,
            zi, wi, zo, hs, lg, a1_s, a1_r, a2_s, a2_r, a3_s, a3_r, h1_s, h1_r, h2_s, h2_r, h3_s, h3_r, lo, la, ag_s, ag_r, du_s, du_r, dl, ct_s, ct_r, st_s, st_r, me_s, me_r, ls_s, ls_r, dg_s, dg_r):
    T, D, V = z_.T, z_.D, z_.V
    PV, ST, PT, SL, SK, NPV, RV, SG = z_.PV, z_.ST, z_.PT, z_.SL, z_.SK, z_.NPV, z_.RV, z_.SG
    OW, OC, OS, RA, AC, AS, AG, NOS, NAS = z_.OW, z_.OC, z_.OS, z_.RA, z_.AC, z_.AS, z_.AG, z_.NOS, z_.NAS
    NS = PT // ST
    d, t = lax.axis_index("dp"), lax.axis_index("tp")
    core, xx, yy = t % 2, (t // 2) % 2, t // 4
    tc, tx, ty = t + 1 - 2 * core, t + 2 - 4 * xx, t + 4 - 8 * yy
    da_, db_ = d + 1 - 2 * (d % 2), 3 - d
    df_ = 3 - da_
    mid = ((d + 1) // 2) % 2 == 1
    end = ((d + 1) // 2) % 2 == 0
    pc, px, py, pa, pbq, pf_ = (d, tc), (d, tx), (d, ty), (da_, t), (db_, t), (df_, t)
    own0 = (d // 3) * OW
    near0 = (da_ // 3) * OW
    far0 = OW - near0

    pair, quad = range(2), range(4)

    def al(x, m):
        return x if isinstance(x, int) else pl.multiple_of(x, m)

    def a8(x):
        return al(x, 8)

    def a16(x):
        return al(x, 16)

    def tof(x):
        return float(x) if isinstance(x, int) else x.astype(F32)

    def rcopy(src, dst, ssem, rsem, dev):
        return pltpu.make_async_remote_copy(src_ref=src, dst_ref=dst, send_sem=ssem, recv_sem=rsem, device_id=dev, device_id_type=pl.DeviceIdType.MESH)

    cp = pltpu.make_async_copy

    bar = pltpu.get_barrier_semaphore()
    for dev in (pc, px, py, pa, pbq, pf_):
        pl.semaphore_signal(bar, inc=1, device_id=dev, device_id_type=pl.DeviceIdType.MESH)
    hsl = cp(h.at[pl.ds(a16(t * SL), SL), :], wr.at[2, :SL, :], hs.at[4])
    hsl.start()

    def hcopy(b):
        return cp(h.at[pl.ds(a16(b * PT), PT), :], unv.at[pl.ds(a16(b * PT), PT), :], hs.at[b])

    for b in quad:
        hcopy(b).start()

    def wcopy(r0, n, slot):
        return cp(wT.at[pl.ds(r0, n), :], wr.at[slot, :n, :], wi.at[slot])

    wcopy(0, PV, 0).start()
    hsl.wait()

    def rms(hb):
        x = hb.astype(F32)
        inv = lax.rsqrt(jnp.mean(x * x, axis=1, keepdims=True) + EPS_NORM)
        return x * inv, inv

    xh, _ = rms(wr[2, :SL, :])
    ub0 = RA + OW - SL
    pb[ub0:ub0 + SL, :] = (xh * gain[...]).astype(BF16).astype(F32)
    sub_iota = lax.broadcasted_iota(jnp.int32, (8, T), 0).astype(F32)
    toff = (t * V).astype(F32)
    lab8[0] = jnp.broadcast_to(lab[...] - toff, (8, T)) - sub_iota
    cntb[0] = jnp.broadcast_to(jnp.sum(msk[...], axis=1, keepdims=True), (8, 128))
    m8[...] = jnp.full((8, T), -jnp.inf, F32)
    s8[...] = jnp.zeros((8, T), F32)
    t8[...] = jnp.zeros((8, T), F32)
    pl.semaphore_wait(bar, 6)

    def urow(tt, u):
        return unf.at[u // 2, pl.ds(a8(tt * SL + (u % 2) * SK), SK), :]

    def zsend(u, dev):
        return rcopy(pb.at[pl.ds(ub0 + (u % 2) * SK, SK), :], urow(t, u), ag_s.at[u, 0], ag_r.at[u, 0], dev)

    def metas(slot, dev):
        return [rcopy(src, dst.at[slot + o], me_s.at[i, slot], me_r.at[i, slot], dev)
                for i, (src, dst, o) in enumerate(((lab, labn, 0), (msk, mskn, 0), (lsev.at[0], lsev, 1)))]

    def ag(u, j):
        tf, tg = (tx, ty) if u % 2 == 0 else (ty, tx)
        pf, pg = (px, py) if u % 2 == 0 else (py, px)
        tfg = tf + tg - t
        who, dev = ((None, None), (t, pf), (t, pg), (tf, pg), (t, pc), (tf, pc), (tg, pc), (tfg, pc))[j]
        return rcopy(urow(who, u), urow(who, u), ag_s.at[u, j], ag_r.at[u, j], dev)

    def cnt2(i):
        return rcopy(cntb.at[i], cntr.at[i], ct_s.at[i], ct_r.at[i], (pa, pbq)[i])

    def lss2(i):
        return rcopy(lsb.at[i], lsr.at[i], ls_s.at[i], ls_r.at[i], (pa, pbq)[i])

    cnt2(0).start()

    @pl.when(mid)
    def _():
        for c in metas(1, pa)[:2] + metas(2, pf_)[:2]:
            c.start()

    @pl.when(end)
    def _():
        for c in metas(0, pbq)[:2]:
            c.start()
        for u in pair:
            zsend(u, pbq).start()

    def e1(u):
        zsend(u, pa).wait_recv()
        for j in (1, 2, 4):
            ag(u, j).start()

    def e23(u):
        ag(u, 1).wait_recv()
        ag(u, 3).start()
        ag(u, 5).start()
        ag(u, 2).wait_recv()
        ag(u, 6).start()

    def e4(u):
        ag(u, 3).wait_recv()
        ag(u, 7).start()

    def ec(_):
        cnt2(0).wait()
        cntb[1] = cntb[0] + cntr[0]
        cnt2(1).start()

    def near(_):
        for u in range(2, 4):
            zsend(u, pa).start()

    def far(_):
        for u in range(4, 6):
            zsend(u, pf_).start()

    def run(evs, names):
        for i in range(0, len(evs), 2):
            names[evs[i]](int(evs[i + 1]))

    enames = dict(i=e1, j=e23, k=e4)
    early = dict(d="i0", g="i1", h="j0")

    def stats(z, n, base, cols):
        labb = lab8[0, :, cols] - tof(base)
        m, s, tg = m8[:, cols], s8[:, cols], t8[:, cols]
        for w0 in range(0, n, 128):
            kk = min(128, n - w0)
            z3 = z[w0:w0 + kk].reshape(kk // 8, 8, ST)
            mn = jnp.maximum(m, jnp.max(z3, axis=0))
            mc = mn * LOG2E
            s = s * jnp.exp2(m * LOG2E - mc) + jnp.sum(jnp.exp2(z3 * LOG2E - mc[None]), axis=0)
            for i in range(kk // 8):
                tg = tg + jnp.where(labb == float(w0 + 8 * i), z3[i], 0.0)
            m = mn
        m8[:, cols], s8[:, cols], t8[:, cols] = m, s, tg

    def zout(tb, r0, n):
        return cp(zr.at[tb, :n, :], zh.at[tb, pl.ds(r0, n), :], zo.at[tb])

    def fwd_pieces(ws, tbs, r0, n):
        for tb in tbs:
            for k in range(NS):
                cols = pl.ds(al(tb * PT + k * ST, ST), ST)
                z = lax.dot_general(wr[ws, :n, :], uv[cols, :], NT, preferred_element_type=F32)
                zr[tb, :n, pl.ds(k * ST, ST)] = z
                stats(z, n, r0, cols)
            zout(tb, r0, n).start()

    @pl.loop(0, NPV * 2)
    def _(q):
        v, half = q // 2, q % 2
        r0 = a16(v * PV)
        ws = v % 2

        @pl.when(half == 0)
        def _():
            wcopy(r0, PV, ws).wait()

            @pl.when(v + 1 < NPV)
            def _():
                wcopy(a16(r0 + PV), PV, 1 - ws).start()

        @pl.when(v == 0)
        def _():
            for k in pair:
                tb = 2 * half + k
                hcopy(tb).wait()
                rows = pl.ds(a16(tb * PT), PT)
                xb, _ = rms(unv[rows, :])
                uv[rows, :] = (xb * gain[...]).astype(BF16)

        @pl.when(v > 0)
        def _():
            for k in pair:
                zout(2 * half + k, 0, PV).wait()

        fwd_pieces(ws, (2 * half, 2 * half + 1), r0, PV)

        def at(i):
            return (half == 1) & (v == min(i, NPV - 1))

        @pl.when(at(1))
        def _():
            ec(0)

        @pl.when(mid & at(6))
        def _():
            near(0)

        for ch, evs in early.items():
            @pl.when(end & at(ord(ch) - ord("a")))
            def _():
                run(evs, enames)

    wcopy(NPV * PV, RV, 2).start()
    wcopy(NPV * PV, RV, 2).wait()

    @pl.loop(0, 4)
    def _(tb):
        zout(tb, 0, PV).wait()
        fwd_pieces(2, (tb,), NPV * PV, RV)

    m = jnp.max(m8[...], axis=0, keepdims=True)
    s = jnp.sum(s8[...] * jnp.exp(m8[...] - m), axis=0, keepdims=True)
    sts[0, 0:1, :] = m + jnp.log(s)
    sts[0, 1:2, :] = jnp.sum(t8[...], axis=0, keepdims=True)
    for r, dev in enumerate((pc, px, py)):
        c = rcopy(sts.at[r], strv.at[r], st_s.at[r], st_r.at[r], dev)
        c.start()
        c.wait()
        a, b = sts[r, 0:1, :], strv[r, 0:1, :]
        hi = jnp.maximum(a, b)
        sts[r + 1, 0:1, :] = hi + jnp.log(jnp.exp(a - hi) + jnp.exp(b - hi))
        sts[r + 1, 1:2, :] = sts[r, 1:2, :] + strv[r, 1:2, :]
    lse, tgt = sts[3, 0:1, :], sts[3, 1:2, :]
    lsev[0] = lse * LOG2E
    cnt2(1).wait()
    cnt = (cntb[1] + cntr[1])[0:1, 0:1]
    mnv[0] = msk[...] / cnt
    lsb[0] = jnp.broadcast_to(jnp.sum(msk[...] * (lse - tgt), axis=1, keepdims=True), (8, 128))

    @pl.when(mid)
    def _():
        metas(1, pa)[2].start()
        metas(2, pf_)[2].start()
        far(0)

    @pl.when(end)
    def _():
        metas(0, pbq)[2].start()
        run("i2j1k0", enames)

    lss2(0).start()
    for tb in quad:
        zout(tb, 0, RV).wait()

    def gmat(z, who, base, cols):
        one = 0 if who is None else 1
        labb = lab8[one, :, cols] - tof(base)
        lse2 = lsev[0 if who is None else who + 1, :, cols]
        mn = jnp.broadcast_to(mnv[one, :, cols], (8, ST))
        p = jnp.exp2(z * LOG2E - lse2)
        rows = []
        for i in range(z.shape[0] // 8):
            pi = p[8 * i:8 * i + 8]
            rows.append(jnp.where(labb == float(8 * i), pi - 1.0, pi) * mn)
        return jnp.concatenate(rows, axis=0).astype(BF16)

    def arow(i):
        return pl.ds(a8(i * AS), AS)

    def awr(i):
        return dw.at[pl.ds(a8(2 * OW + i * AS), AS), :]

    def a1(i):
        return rcopy(pb.at[arow(i), :], rb.at[arow(i), :], a1_s.at[i], a1_r.at[i], pa)

    def a2(i):
        return rcopy(pb.at[arow(i), :], rc.at[arow(i), :], a2_s.at[i], a2_r.at[i], pbq)

    def a3(i):
        return rcopy(pb.at[arow(i), :], awr(i), a3_s.at[i], a3_r.at[i], pa)

    def alocal(i):
        return cp(pb.at[arow(i), :], awr(i), la.at[i])

    def grab(src, i):
        for o in range(0, AS, AG):
            n = min(AG, AS - o)
            rows = pl.ds(a8(i * AS + o), n)
            c = cp(src.at[rows, :], stg.at[:n, :], lg.at[0])
            c.start()
            c.wait()
            pb[rows, :] = pb[rows, :] + stg[:n, :]

    def ev_a1(i):
        a1(i).wait_recv()
        grab(rb, i)
        a2(i).start()

    def ev_a2(i):
        a2(i).wait()
        grab(rc, i)
        alocal(i).start()
        a3(i).start()

    def drow(base, i):
        return dw.at[pl.ds(a8(base + i * OS), OS), :]

    def prow(i):
        return pb.at[pl.ds(a8(RA + i * OS), OS), :]

    def h1(i):
        return rcopy(prow(i), drow(own0, i), h1_s.at[i], h1_r.at[i], pa)

    def h2(i):
        return rcopy(drow(near0, i), drow(near0, i), h2_s.at[i], h2_r.at[i], pbq)

    def h3(i):
        return rcopy(drow(far0, i), drow(far0, i), h3_s.at[i], h3_r.at[i], pa)

    def hop(i):
        h1(i).wait_recv()
        h2(i).start()
        if not isinstance(i, int) or i > 0:
            h2(i - 1).wait_recv()
            h3(i - 1).start()

    def hlocal(i):
        return cp(prow(i), drow(own0, i), lo.at[i])

    H = SG // 2
    k0 = core * (4 * SG)

    def lev(k):
        fb, sb = (xx, yy) if k == 0 else (yy, xx)
        pf, ps = (px, py) if k == 0 else (py, px)
        k1 = k * 2 * SG + fb * SG
        return pf, ps, k1, k * 2 * SG + (1 - fb) * SG, k1 + sb * H, k1 + (1 - sb) * H

    def ducopy(g, j, k=0):
        pf, ps, k1, o1, k2, o2 = lev(k)
        b = g % 2
        base = g * PT + k0
        sems = (du_s.at[g, j, k], du_r.at[g, j, k])
        if j == 0:
            return rcopy(da.at[b, pl.ds(a8(4 * SG - k0), 4 * SG), :], dub0.at[g], *sems, pc)
        if j == 1:
            return rcopy(da2.at[b, pl.ds(a8(o1), SG), :], dub1.at[g, k], *sems, pf)
        if j == 2:
            return rcopy(da2.at[b, pl.ds(a8(o2), H), :], dub2.at[g, k], *sems, ps)
        if j == 3:
            return rcopy(dhs.at[b, k], dh.at[pl.ds(a8(base + k2), H), :], *sems, ps)
        r, n, dev = ((k1, SG, pf), (0, 4 * SG, pc))[j - 4]
        r = dh.at[pl.ds(a8(base + r), n), :]
        return rcopy(r, r, *sems, dev)

    def add_in(buf, g, src, k, k2, n):
        @pl.loop(0, n // SG)
        def _(i):
            c = cp(buf.at[pl.ds(a8(i * SG), SG), :], stg.at[:SG, :], lg.at[1])
            c.start()
            c.wait()
            da2[g % 2, pl.ds(a8(k2 + i * SG), SG), :] = src[g % 2, pl.ds(a8(k + i * SG), SG), :] + stg[:SG, :]

    def d2(g):
        ducopy(g, 0).wait_recv()
        for k in pair:
            if g >= 2:
                ducopy(g - 2, 1, k).wait_send()
                ducopy(g - 2, 2, k).wait_send()
        add_in(dub0.at[g], g, da, k0, 0, 4 * SG)
        for k in pair:
            ducopy(g, 1, k).start()

    def d3(g):
        for k in pair:
            ducopy(g, 1, k).wait_recv()
            add_in(dub1.at[g, k], g, da2, lev(k)[2], lev(k)[2], SG)
            ducopy(g, 2, k).start()

    def dhlocal(g, k):
        return cp(dhs.at[g % 2, k], dh.at[pl.ds(a8(g * PT + k0 + lev(k)[4]), H), :], dl.at[g, k])

    def d4(g):
        for k in pair:
            k2 = lev(k)[4]
            ch = cp(h.at[pl.ds(a8(g * PT + k0 + k2), H), :], hst, lg.at[2])
            ch.start()
            ducopy(g, 2, k).wait_recv()
            c = cp(dub2.at[g, k], stg.at[:H, :], lg.at[1])
            c.start()
            c.wait()
            if g >= 2:
                ducopy(g - 2, 3, k).wait_send()
            ch.wait()
            xb, inv = rms(hst[...])
            du = da2[g % 2, pl.ds(a8(k2), H), :] + stg[:H, :]
            part = jnp.sum((du * xb).reshape(H // 8, 8, D), axis=0)
            dgb[0] = part if g == 0 and k == 0 else dgb[0] + part
            a = du * gain[...]
            dhs[g % 2, k] = inv * (a - xb * jnp.mean(a * xb, axis=1, keepdims=True))
            dhlocal(g, k).start()
            ducopy(g, 3, k).start()

    def d5(g):
        for k in pair:
            ducopy(g, 3, k).wait_recv()
            dhlocal(g, k).wait()
            ducopy(g, 4, k).start()

    def d6(g):
        for k in pair:
            ducopy(g, 4, k).wait_recv()
        ducopy(g, 5).start()

    dgdev = (pc, px, py, pa, pbq)

    def dgc(r):
        return rcopy(dgb.at[r], dgr.at[r], dg_s.at[r], dg_r.at[r], dgdev[r])

    def ev_dg(r):
        if r > 0:
            dgc(r - 1).wait()
            dgb[r] = dgb[r - 1] + dgr[r - 1]
        if r < 5:
            dgc(r).start()

    def ev_ls():
        lss2(0).wait()
        lsb[1] = lsb[0] + lsr[0]
        lss2(1).start()

    dnames = dict(a=d2, b=d3, c=d4, d=d5, e=d6, g=ev_dg)
    mnames = dict(p=ev_a1, q=ev_a2, h=hop)
    duev = dict(m1="a0", m2="b0a1", m3="c0a2", f3="b1")
    muev = dict(m1="p0", f1="p1", m2="q0p2", f2="q1", m3="p3q2")

    def poll(kind, idx):
        for i in quad:
            key = kind + str(i)
            if key in duev:
                @pl.when(idx == i)
                def _():
                    run(duev[key], dnames)
            if key in muev:
                @pl.when((idx == i) & mid)
                def _():
                    run(muev[key], mnames)

    def zin(tb, r0, n, slot):
        return cp(zh.at[tb, pl.ds(r0, n), :], zr.at[slot, :n, :], zi.at[slot])

    def uin(sh, b):
        n = PT // 2
        return cp(unf.at[sh, pl.ds(a8(b * n), n), :], zr.at[b % 4, :n, :], zi.at[b % 4])

    def convert(sh):
        for k in pair:
            for j in range(4, 8):
                ag_wait = rcopy(unf.at[0, :SK, :], unf.at[0, :SK, :], ag_s.at[2 * sh + k, j], ag_r.at[2 * sh + k, j], pc)
                ag_wait.wait_recv()
        for i, dst in enumerate((labn, mskn, lsev)):
            rcopy(dst.at[0], dst.at[0], me_s.at[i, sh], me_r.at[i, sh], pa).wait_recv()
        mnv[1] = mskn[sh] / cnt
        lab8[1] = jnp.broadcast_to(labn[sh] - toff, (8, T)) - sub_iota
        for b in quad:
            uin(sh, b).start()

    def own_start(g0, n):
        for tb in quad:
            zin(tb, g0, n, tb).start()

    def chunk_own(r0, g0, n, more):
        rows = pl.ds(r0, n)
        pb[rows, :] = jnp.zeros((n, D), F32)

        @pl.loop(0, 4)
        def _(tb):
            zin(tb, g0, n, tb).wait()
            gs = []
            for k in range(NS):
                gs.append(gmat(zr[tb, :n, pl.ds(k * ST, ST)], None, g0, pl.ds(al(tb * PT + k * ST, ST), ST)))
            g = jnp.concatenate(gs, axis=1)

            @pl.when(more)
            def _():
                zin(tb, a8(g0 + n), n, tb).start()

            pb[rows, :] += jnp.dot(g, uv[pl.ds(a16(tb * PT), PT), :], preferred_element_type=F32)

    def chunk_far(r0, g0, n, sh, first):
        wcopy(g0, n, 0).start()
        wcopy(g0, n, 0).wait()
        rows = pl.ds(r0, n)

        @pl.loop(0, 2)
        def _(q):
            @pl.when(first)
            def _():
                for b in quad:
                    uin(sh, 4 * q + b).wait()
                    unv[pl.ds(a16((4 * q + b) * (PT // 2)), PT // 2), :] = zr[b, :PT // 2, :].astype(BF16)

                @pl.when(q == 0)
                def _():
                    for b in range(4, 8):
                        uin(sh, b).start()

            for j in pair:
                gs = []
                for k in range(NS):
                    cols = pl.ds(al((2 * q + j) * PT + k * ST, ST), ST)
                    z = lax.dot_general(wr[0, :n, :], unv[cols, :], NT, preferred_element_type=F32)
                    gs.append(gmat(z, sh, g0, cols))
                g = jnp.concatenate(gs, axis=1)
                pb[rows, :] += jnp.dot(g, unv[pl.ds(a16((2 * q + j) * PT), PT), :], preferred_element_type=F32)

    def du_piece(b, tb, v, r0, n):
        for k in range(NS):
            g = gmat(zr[v % 4, :n, pl.ds(k * ST, ST)], None, r0, pl.ds(al(tb * PT + k * ST, ST), ST))
            da[b, pl.ds(k * ST, ST), :] += lax.dot_general(g, wr[v % 3, :n, :], TN, preferred_element_type=F32)

    def du_block(tb):
        b = tb % 2

        def pz(v, n):
            return zin(tb, a16(v * PV), n, v % 4)

        def pw(v, n):
            return wcopy(a16(v * PV), n, v % 3)

        for g in range(2, 4):
            @pl.when(tb == g)
            def _():
                ducopy(g - 2, 0).wait_send()

        for v in pair:
            pz(v, PV).start()
            pw(v, PV).start()
        pz(2, PV).start()
        da[b] = jnp.zeros((PT, D), F32)

        @pl.loop(0, NPV)
        def _(v):
            pz(v, PV).wait()
            pw(v, PV).wait()
            for o, f in ((3, pz), (2, pw)):
                @pl.when(v + o < NPV)
                def _():
                    f(v + o, PV).start()

                @pl.when(v + o == NPV)
                def _():
                    f(NPV, RV).start()

            du_piece(b, tb, v, v * PV, PV)

            @pl.when(v == NPV // 2)
            def _():
                poll("m", tb)

        pz(NPV, RV).wait()
        pw(NPV, RV).wait()
        du_piece(b, tb, NPV, NPV * PV, RV)
        poll("f", tb)
        for g in quad:
            @pl.when(tb == g)
            def _():
                ducopy(g, 0).start()

    shev = dict(s00="j3i5", s01="k2", s03="j4", s04="k3", s11="j5", s12="k4", s14="k5")

    own_start(2 * OW, AC)

    @pl.loop(0, RA // AC)
    def _(c):
        chunk_own(a8(c * AC), a8(2 * OW + c * AC), AC, c + 1 < RA // AC)

        for i, evs in enumerate(("", "", "i3j2")):
            if evs:
                @pl.when(end & (c == i))
                def _():
                    run(evs, enames)

        @pl.when(end)
        def _():
            for s in range(AC // AS):
                a1(c * (AC // AS) + s).start()

    @pl.when(end)
    def _():
        own_start(a8(own0), OC)

        @pl.loop(0, OW // OC)
        def _(c):
            @pl.when(c == (ub0 - RA) // OC)
            def _():
                for u in pair:
                    zsend(u, pbq).wait_send()

            chunk_own(a8(RA + c * OC), a8(own0 + c * OC), OC, c + 1 < OW // OC)
            for i, evs in enumerate(("", "", "k1i4", "", "")):
                if evs:
                    @pl.when(c == i)
                    def _():
                        run(evs, enames)

        @pl.loop(0, 3)
        def _(sh):
            convert(sh)

            @pl.loop(0, OW // OC)
            def _(c):
                chunk_far(a8(RA + c * OC), a8(own0 + c * OC), OC, sh, c == 0)
                for x, evs in shev.items():
                    @pl.when((sh == int(x[1])) & (c == int(x[2])))
                    def _():
                        run(evs, enames)

                @pl.when(sh == 2)
                def _():
                    for s in range(OC // OS):
                        i = c * (OC // OS) + s
                        hlocal(i).start()
                        h1(i).start()

    @pl.loop(0, 4)
    def _(tb):
        du_block(tb)

    @pl.when(mid)
    def _():
        run("p4q3c1a3b2d0p5q4c2b3d1e0q5c3g0d2g1e1h0g2d3e2h1e3h2", {**dnames, **mnames})

        @pl.loop(3, NOS)
        def _(i):
            hop(i)

        h2(NOS - 1).wait_recv()
        h3(NOS - 1).start()

    @pl.when(end)
    def _():
        run("c1a3b2d0c2b3d1e0c3g0d2g1e1g2d3e2e3", dnames)

    run("g3g4", dnames)
    ev_ls()
    run("g5", dnames)

    dg[...] = jnp.sum(dgb[5], axis=0, keepdims=True)
    lss2(1).wait()
    loss[...] = (lsb[1] + lsr[1]) / cnt
    for g in quad:
        ducopy(g, 5).wait()
        for k in pair:
            ducopy(g, 4, k).wait_send()
            if g >= 2:
                for j in (1, 2, 3):
                    ducopy(g, j, k).wait_send()
        if g >= 2:
            ducopy(g, 0).wait_send()

    @pl.when(mid)
    def _():
        for u in range(2, 6):
            zsend(u, pa).wait_send()
        for c in metas(1, pa) + metas(2, pf_):
            c.wait_send()

        @pl.loop(0, NAS)
        def _(i):
            a3(i).wait_send()
            alocal(i).wait()

        @pl.loop(0, NOS)
        def _(i):
            h2(i).wait_send()
            h3(i).wait_send()

    @pl.when(end)
    def _():
        for u in range(6):
            for j in range(1, 8):
                ag(u, j).wait_send()
        for c in metas(0, pbq):
            c.wait_send()

        @pl.loop(0, NAS)
        def _(i):
            a1(i).wait_send()
            a3(i).wait_recv()

        @pl.loop(0, NOS)
        def _(i):
            hlocal(i).wait()
            h1(i).wait_send()
            h3(i).wait_recv()


def _call(z_, h, lab, msk, gain, wT):
    T, D, V, RA, SG, PT, PV, OW = z_.T, z_.D, z_.V, z_.RA, z_.SG, z_.PT, z_.PV, z_.OW
    vm = pl.BlockSpec(memory_space=pltpu.VMEM)
    hb = pl.BlockSpec(memory_space=pl.ANY)
    outs = [jax.ShapeDtypeStruct(s, F32) for s in (
        (V, D), (T, D), (1, D), (8, 128), (4, V, PT), (3, T, D), (RA, D), (RA, D), (4, 4 * SG, D), (4, 2, SG, D), (4, 2, SG // 2, D))]
    bufs = [((T, D), BF16), ((T, D), BF16), ((RA + OW, D), F32), ((4, PV, PT), F32), ((3, PV, D), BF16), ((2, PT, D), F32), ((2, PT // 2, D), F32),
            ((max(z_.AG, SG), D), F32), ((SG // 2, D), BF16), ((2, 2, SG // 2, D), F32)]
    row = ((8, T),) * 3 + ((2, 8, T),) + tuple((int(k), 1, T) for k in "4233") + ((4, 2, T), (3, 2, T))
    tiles = ((2, 8, 128),) * 4 + ((6, 8, D), (5, 8, D))
    bufs += [(s, F32) for s in row + tiles]
    pairs = ((z_.NAS,),) * 6 + ((z_.NOS,),) * 6
    def shapes(text):
        return tuple(tuple(int(c) for c in w) for w in text.split("-"))

    sems = shapes("4-4-4-5-3") + pairs + ((z_.NOS,), (z_.NAS,)) + shapes("68-68-462-462-42-2-2-3-3-33-33-2-2-5-5")
    return pl.pallas_call(
        functools.partial(_kernel, z_),
        out_shape=outs,
        in_specs=[hb, vm, vm, vm, hb],
        out_specs=[hb, hb, vm, vm] + [hb] * (len(outs) - 4),
        scratch_shapes=[pltpu.VMEM(s, t) for s, t in bufs] + [pltpu.SemaphoreType.DMA(s) for s in sems],
        compiler_params=pltpu.CompilerParams(collective_id=0, has_side_effects=True, vmem_limit_bytes=1023 * 65536),
        name="lm_head",
    )(h, lab, msk, gain, wT)


def make(mesh, z_):
    def local_step(hidden, labels, loss_mask, norm_gain, w_shard):
        h = hidden.reshape(z_.T, z_.D)
        lab = labels.reshape(1, z_.T).astype(F32)
        msk = loss_mask.reshape(1, z_.T).astype(F32)
        gain = norm_gain.astype(F32).reshape(1, z_.D)
        o = _call(z_, h, lab, msk, gain, w_shard.T)
        dw, dh, dg, loss = o[:4]
        return loss[0, 0], dh.astype(BF16).reshape(hidden.shape), dg.reshape(z_.D), dw.T

    return jax.shard_map(local_step, mesh=mesh, in_specs=(P("dp", None, None), P("dp", None), P("dp", None), P(None), P(None, "tp")), out_specs=(P(), P("dp", None, None), P(None), P(None, "tp")), check_vma=False)


def solution(mesh):
    return make(mesh, Sizes(4096, 1024, 6288, 512, 2400, 480, 120, 496, 248, 256))
```

time: 1390 us -> 585 us (0.42)
  waiting for transfers between devices: 967 us -> 0 us
  Pallas kernels: 0 us -> 549 us
  matrix products: 191 us -> 0 us
  other arithmetic: 124 us -> 11.8 us
  blocking collectives: 73.1 us -> 0 us
  between operations: 16.5 us -> 0.64 us
    psum x2 -> x0, waiting for transfers between devices: 967 us -> none  [the longest x1 817 us: local_step(): d_w_out = lax.psum(dw_part, 'dp')]
    pallas_call x0 -> x1, Pallas kernels: none -> 549 us  [_call(): pl.pallas_call(functools.partial(_kernel, z_), out_shape=outs, in_specs=[...]
    dot_general x3 -> x0, matrix products: 191 us -> none  [the longest x1 65 us: local_step(): logits = jnp.dot(u_tok, w_shard, preferred_element_type=jnp.float32)]
    convert_element_type x4 -> x1, other arithmetic: 71.5 us -> 9.07 us  [local_step(): dh.astype(BF16).reshape(hidden.shape)]
    reduce_sum x4 -> x0, other arithmetic: 48.6 us -> none  [the longest x1 32.2 us: local_step(): jnp.sum(shifted, axis=1, keepdims=True)]
    psum x3 -> x0, blocking collectives: 47.5 us -> none  [the longest x1 22.4 us: local_step(): full_stats = lax.psum(part_stats, 'tp')]
    pmax x1 -> x0, blocking collectives: 25.6 us -> none  [local_step(): glob_max = lax.pmax(jnp.max(logits, axis=1, keepdims=True), 'tp')]
  transfers between devices with their start and end apart: 2 -> 0, of which waited for: 2 -> 0; matrix products, arithmetic and copies ran while one was open for 6% -> 0% of each run, Pallas kernels for 0% -> 0%
where the time goes in v1:
time: 585 us; the launch traced here: 583 us
  Pallas kernels  549 us (94%)
  local copies, waits for them, and re-layouts  21.1 us (4%)
  other arithmetic  11.8 us (2%)
    pallas_call x1, Pallas kernels, _call(): pl.pallas_call(functools.partial(_kernel, z_), out_shape=outs, in_specs=[...  549 us
    unnamed x6, local copies, waits for them, and re-layouts  19.9 us

profile of v1, /device:TPU:0, one launch (start us, length us, event | category | flops | bytes accessed | tf_op | source)
XLA Modules:
  0.0 582.5 jit_solution(13816047833338593398)
XLA Ops:
  0.6 1.3 reshape.55
  1.9 0.7 convert_bitcast_fusion.1
  2.6 0.6 copy.9
  3.3 0.7 convert_bitcast_fusion
  4.0 0.6 copy.10
  4.6 549.0 %lm_head.1 = (f32[6288,1024]{1,0:T(8,128)}, f32[4096,1024]{1,0:T(8,128)}, f32[1,1024]{1,0:T(1,128)}, f32[8,128]{1,0:T(8,128)}, f32[4,6288,1024]{2,1,0:T(8,128)},...) custom-call(bf16[4096,1024]{1,0:T(8,128)(2,1)} %bitcast.18, ...), custom_call_target="tpu_custom_call" | custom-call | tf_op jit(solution)/shard_map/lm_head/pallas_call | solution.py:755
  553.6 1.2 slice.3
  554.8 0.0 copy-start
  554.8 9.1 %convert_element_type.18 = bf16[4096,1024]{1,0:T(8,128)(2,1)} convert(f32[4096,1024]{1,0:T(8,128)} %get-tuple-element.9) | non-fusion elementwise | flops 4194304 | bytes 25165824 | tf_op jit(solution)/shard_map/convert_element_type | solution.py:774
  563.9 0.0 copy-done
  563.9 0.6 copy.13
  564.5 18.1 %copy.14 = f32[1024,6288]{0,1:T(8,128)} copy(f32[1024,6288]{0,1:T(8,128)} %bitcast.15) | data formatting | bytes 51511296
Async XLA Ops:
  554.8 9.1 %copy-start = (f32[1,1024]{1,0:T(1,128)S(1)}, f32[1,1024]{1,0:T(1,128)}, u32[]{:S(2)}) copy-start(f32[1,1024]{1,0:T(1,128)} %get-tuple-element.10) | copy-start | bytes 12292

commit v2 on v1

--- a/solution.py
+++ b/solution.py
@@ -33,7 +33,7 @@
 
 
 def _kernel(z_, h, lab, msk, gain, wT, dw, dh, dg, loss, zh, unf, rb, rc, dub0, dub1, dub2,
-            uv, unv, pb, zr, wr, da, da2, stg, hst, dhs, m8, s8, t8, lab8, lsev, mnv, mskn, labn, sts, strv, cntb, cntr, lsb, lsr, dgb, dgr,
+            uv, unv, pb, zr, wr, da, da2, stg, hst, dhs, m8, s8, t8, lab8, lsev, mnv, ltv, mskn, labn, sts, strv, cntb, cntr, lsb, lsr, dgb, dgr,
             zi, wi, zo, hs, lg, a1_s, a1_r, a2_s, a2_r, a3_s, a3_r, h1_s, h1_r, h2_s, h2_r, h3_s, h3_r, lo, la, ag_s, ag_r, du_s, du_r, dl, ct_s, ct_r, st_s, st_r, me_s, me_r, ls_s, ls_r, dg_s, dg_r):
     T, D, V = z_.T, z_.D, z_.V
     PV, ST, PT, SL, SK, NPV, RV, SG = z_.PV, z_.ST, z_.PT, z_.SL, z_.SK, z_.NPV, z_.RV, z_.SG
@@ -142,19 +142,26 @@
         for u in pair:
             zsend(u, pbq).start()
 
+    def e1f(u):
+        zsend(u, pa).wait_recv()
+        ag(u, 1).start()
+
+    def e1r(u):
+        ag(u, 2).start()
+        ag(u, 4).start()
+
     def e1(u):
-        zsend(u, pa).wait_recv()
-        for j in (1, 2, 4):
-            ag(u, j).start()
+        e1f(u)
+        e1r(u)
 
     def e23(u):
         ag(u, 1).wait_recv()
         ag(u, 3).start()
         ag(u, 5).start()
+
+    def e4(u):
         ag(u, 2).wait_recv()
         ag(u, 6).start()
-
-    def e4(u):
         ag(u, 3).wait_recv()
         ag(u, 7).start()
 
@@ -175,8 +182,8 @@
         for i in range(0, len(evs), 2):
             names[evs[i]](int(evs[i + 1]))
 
-    enames = dict(i=e1, j=e23, k=e4)
-    early = dict(d="i0", g="i1", h="j0")
+    enames = dict(i=e1, j=e23, k=e4, m=e1f, n=e1r)
+    early = dict(d="i0", g="i1", h="j0", k="m2")
 
     def stats(z, n, base, cols):
         labb = lab8[0, :, cols] - tof(base)
@@ -204,44 +211,42 @@
                 stats(z, n, r0, cols)
             zout(tb, r0, n).start()
 
-    @pl.loop(0, NPV * 2)
-    def _(q):
-        v, half = q // 2, q % 2
+    @pl.loop(0, NPV)
+    def _(v):
         r0 = a16(v * PV)
         ws = v % 2
-
-        @pl.when(half == 0)
+        wcopy(r0, PV, ws).wait()
+
+        @pl.when(v + 1 < NPV)
         def _():
-            wcopy(r0, PV, ws).wait()
-
-            @pl.when(v + 1 < NPV)
-            def _():
-                wcopy(a16(r0 + PV), PV, 1 - ws).start()
-
-        @pl.when(v == 0)
-        def _():
-            for k in pair:
-                tb = 2 * half + k
-                hcopy(tb).wait()
-                rows = pl.ds(a16(tb * PT), PT)
-                xb, _ = rms(unv[rows, :])
-                uv[rows, :] = (xb * gain[...]).astype(BF16)
-
-        @pl.when(v > 0)
-        def _():
-            for k in pair:
-                zout(2 * half + k, 0, PV).wait()
-
-        fwd_pieces(ws, (2 * half, 2 * half + 1), r0, PV)
+            wcopy(a16(r0 + PV), PV, 1 - ws).start()
+
+        for half in pair:
+            tbs = (2 * half, 2 * half + 1)
+
+            @pl.when(v == 0)
+            def _():
+                for tb in tbs:
+                    hcopy(tb).wait()
+                    rows = pl.ds(tb * PT, PT)
+                    xb, _ = rms(unv[rows, :])
+                    uv[rows, :] = (xb * gain[...]).astype(BF16)
+
+            @pl.when(v > 0)
+            def _():
+                for tb in tbs:
+                    zout(tb, 0, PV).wait()
+
+            fwd_pieces(ws, tbs, r0, PV)
 
         def at(i):
-            return (half == 1) & (v == min(i, NPV - 1))
+            return v == min(i, NPV - 1)
 
         @pl.when(at(1))
         def _():
             ec(0)
 
-        @pl.when(mid & at(6))
+        @pl.when(mid & at(5))
         def _():
             near(0)
 
@@ -275,6 +280,7 @@
     cnt2(1).wait()
     cnt = (cntb[1] + cntr[1])[0:1, 0:1]
     mnv[0] = msk[...] / cnt
+    ltv[0] = lsev[0] - jnp.log2(mnv[0])
     lsb[0] = jnp.broadcast_to(jnp.sum(msk[...] * (lse - tgt), axis=1, keepdims=True), (8, 128))
 
     @pl.when(mid)
@@ -286,7 +292,7 @@
     @pl.when(end)
     def _():
         metas(0, pbq)[2].start()
-        run("i2j1k0", enames)
+        run("n2j1k0", enames)
 
     lss2(0).start()
     for tb in quad:
@@ -295,13 +301,12 @@
     def gmat(z, who, base, cols):
         one = 0 if who is None else 1
         labb = lab8[one, :, cols] - tof(base)
-        lse2 = lsev[0 if who is None else who + 1, :, cols]
         mn = jnp.broadcast_to(mnv[one, :, cols], (8, ST))
-        p = jnp.exp2(z * LOG2E - lse2)
+        pm = jnp.exp2(z * LOG2E - ltv[one, :, cols])
         rows = []
         for i in range(z.shape[0] // 8):
-            pi = p[8 * i:8 * i + 8]
-            rows.append(jnp.where(labb == float(8 * i), pi - 1.0, pi) * mn)
+            pi = pm[8 * i:8 * i + 8]
+            rows.append(jnp.where(labb == float(8 * i), pi - mn, pi))
         return jnp.concatenate(rows, axis=0).astype(BF16)
 
     def arow(i):
@@ -501,6 +506,7 @@
         for i, dst in enumerate((labn, mskn, lsev)):
             rcopy(dst.at[0], dst.at[0], me_s.at[i, sh], me_r.at[i, sh], pa).wait_recv()
         mnv[1] = mskn[sh] / cnt
+        ltv[1] = lsev[sh + 1] - jnp.log2(mnv[1])
         lab8[1] = jnp.broadcast_to(labn[sh] - toff, (8, T)) - sub_iota
         for b in quad:
             uin(sh, b).start()
@@ -607,7 +613,7 @@
             def _():
                 ducopy(g, 0).start()
 
-    shev = dict(s00="j3i5", s01="k2", s03="j4", s04="k3", s11="j5", s12="k4", s14="k5")
+    shev = dict(s00="j3i5", s02="j4k2", s04="k3", s11="j5", s14="k4k5")
 
     own_start(2 * OW, AC)
 
@@ -615,7 +621,7 @@
     def _(c):
         chunk_own(a8(c * AC), a8(2 * OW + c * AC), AC, c + 1 < RA // AC)
 
-        for i, evs in enumerate(("", "", "i3j2")):
+        for i, evs in enumerate(("", "", "i3")):
             if evs:
                 @pl.when(end & (c == i))
                 def _():
@@ -638,7 +644,7 @@
                     zsend(u, pbq).wait_send()
 
             chunk_own(a8(RA + c * OC), a8(own0 + c * OC), OC, c + 1 < OW // OC)
-            for i, evs in enumerate(("", "", "k1i4", "", "")):
+            for i, evs in enumerate(("j2", "", "k1i4", "", "")):
                 if evs:
                     @pl.when(c == i)
                     def _():
@@ -669,9 +675,9 @@
 
     @pl.when(mid)
     def _():
-        run("p4q3c1a3b2d0p5q4c2b3d1e0q5c3g0d2g1e1h0g2d3e2h1e3h2", {**dnames, **mnames})
-
-        @pl.loop(3, NOS)
+        run("p4q3c1a3b2d0p5q4c2b3d1q5e0h0c3g0h1d2g1h2e1h3g2d3h4e2h5e3", {**dnames, **mnames})
+
+        @pl.loop(6, NOS)
         def _(i):
             hop(i)
 
@@ -744,7 +750,7 @@
         (V, D), (T, D), (1, D), (8, 128), (4, V, PT), (3, T, D), (RA, D), (RA, D), (4, 4 * SG, D), (4, 2, SG, D), (4, 2, SG // 2, D))]
     bufs = [((T, D), BF16), ((T, D), BF16), ((RA + OW, D), F32), ((4, PV, PT), F32), ((3, PV, D), BF16), ((2, PT, D), F32), ((2, PT // 2, D), F32),
             ((max(z_.AG, SG), D), F32), ((SG // 2, D), BF16), ((2, 2, SG // 2, D), F32)]
-    row = ((8, T),) * 3 + ((2, 8, T),) + tuple((int(k), 1, T) for k in "4233") + ((4, 2, T), (3, 2, T))
+    row = ((8, T),) * 3 + ((2, 8, T),) + tuple((int(k), 1, T) for k in "42233") + ((4, 2, T), (3, 2, T))
     tiles = ((2, 8, 128),) * 4 + ((6, 8, D), (5, 8, D))
     bufs += [(s, F32) for s in row + tiles]
     pairs = ((z_.NAS,),) * 6 + ((z_.NOS,),) * 6

time: 585 us -> 574 us (0.981)
  Pallas kernels: 549 us -> 537 us
    pallas_call x1, Pallas kernels: 549 us -> 537 us  [_call(): pl.pallas_call(functools.partial(_kernel, z_), out_shape=outs, in_specs=[...]
where the time goes in v2:
time: 574 us; the launch traced here: 571 us
  Pallas kernels  537 us (94%)
  local copies, waits for them, and re-layouts  21.1 us (4%)
  other arithmetic  11.8 us (2%)
    pallas_call x1, Pallas kernels, _call(): pl.pallas_call(functools.partial(_kernel, z_), out_shape=outs, in_specs=[...  537 us
    unnamed x6, local copies, waits for them, and re-layouts  19.9 us

profile of v2, /device:TPU:0, one launch (start us, length us, event | category | flops | bytes accessed | tf_op | source)
XLA Modules:
  0.0 570.9 jit_solution(6485051956483315002)
XLA Ops:
  0.6 1.3 reshape.55
  1.9 0.7 convert_bitcast_fusion.1
  2.6 0.6 copy.9
  3.3 0.7 convert_bitcast_fusion
  4.0 0.6 copy.10
  4.6 537.4 %lm_head.1 = (f32[6288,1024]{1,0:T(8,128)}, f32[4096,1024]{1,0:T(8,128)}, f32[1,1024]{1,0:T(1,128)}, f32[8,128]{1,0:T(8,128)}, f32[4,6288,1024]{2,1,0:T(8,128)},...) custom-call(bf16[4096,1024]{1,0:T(8,128)(2,1)} %bitcast.18, ...), custom_call_target="tpu_custom_call" | custom-call | tf_op jit(solution)/shard_map/lm_head/pallas_call | solution.py:761
  542.0 1.2 slice.3
  543.2 0.0 copy-start
  543.2 9.1 %convert_element_type.18 = bf16[4096,1024]{1,0:T(8,128)(2,1)} convert(f32[4096,1024]{1,0:T(8,128)} %get-tuple-element.9) | non-fusion elementwise | flops 4194304 | bytes 25165824 | tf_op jit(solution)/shard_map/convert_element_type | solution.py:780
  552.2 0.0 copy-done
  552.2 0.6 copy.13
  552.8 18.1 %copy.14 = f32[1024,6288]{0,1:T(8,128)} copy(f32[1024,6288]{0,1:T(8,128)} %bitcast.15) | data formatting | bytes 51511296
Async XLA Ops:
  543.2 9.1 %copy-start = (f32[1,1024]{1,0:T(1,128)S(1)}, f32[1,1024]{1,0:T(1,128)}, u32[]{:S(2)}) copy-start(f32[1,1024]{1,0:T(1,128)} %get-tuple-element.10) | copy-start | bytes 12292

commit v3 on v2

--- a/solution.py
+++ b/solution.py
@@ -32,8 +32,8 @@
         self.NOS, self.NAS = own // osub, self.RA // asub
 
 
-def _kernel(z_, h, lab, msk, gain, wT, dw, dh, dg, loss, zh, unf, rb, rc, dub0, dub1, dub2,
-            uv, unv, pb, zr, wr, da, da2, stg, hst, dhs, m8, s8, t8, lab8, lsev, mnv, ltv, mskn, labn, sts, strv, cntb, cntr, lsb, lsr, dgb, dgr,
+def _kernel(z_, h, lab_, msk_, gain, wT, dw, dh, dg, loss, zh, unf, rb, rc, dub0, dub1, dub2,
+            uv, unv, pb, zr, wr, da, da2, stg, hst, dhs, m8, s8, t8, lab, msk, lab8, lsev, mnv, ltv, mskn, labn, sts, strv, cntb, cntr, lsb, lsr, dgb, dgr,
             zi, wi, zo, hs, lg, a1_s, a1_r, a2_s, a2_r, a3_s, a3_r, h1_s, h1_r, h2_s, h2_r, h3_s, h3_r, lo, la, ag_s, ag_r, du_s, du_r, dl, ct_s, ct_r, st_s, st_r, me_s, me_r, ls_s, ls_r, dg_s, dg_r):
     T, D, V = z_.T, z_.D, z_.V
     PV, ST, PT, SL, SK, NPV, RV, SG = z_.PV, z_.ST, z_.PT, z_.SL, z_.SK, z_.NPV, z_.RV, z_.SG
@@ -93,6 +93,10 @@
         inv = lax.rsqrt(jnp.mean(x * x, axis=1, keepdims=True) + EPS_NORM)
         return x * inv, inv
 
+    n = lab_.shape[1]
+    for b in range(T // n):
+        lab[:, pl.ds(b * n, n)] = lab_[pl.ds(b, 1), :].astype(F32)
+        msk[:, pl.ds(b * n, n)] = msk_[pl.ds(b, 1), :].astype(F32)
     xh, _ = rms(wr[2, :SL, :])
     ub0 = RA + OW - SL
     pb[ub0:ub0 + SL, :] = (xh * gain[...]).astype(BF16).astype(F32)
@@ -476,7 +480,7 @@
 
     dnames = dict(a=d2, b=d3, c=d4, d=d5, e=d6, g=ev_dg)
     mnames = dict(p=ev_a1, q=ev_a2, h=hop)
-    duev = dict(m1="a0", m2="b0a1", m3="c0a2", f3="b1")
+    duev = dict(m1="a0", m2="b0a1", m3="c0a2", f3="b1d0")
     muev = dict(m1="p0", f1="p1", m2="q0p2", f2="q1", m3="p3q2")
 
     def poll(kind, idx):
@@ -675,7 +679,7 @@
 
     @pl.when(mid)
     def _():
-        run("p4q3c1a3b2d0p5q4c2b3d1q5e0h0c3g0h1d2g1h2e1h3g2d3h4e2h5e3", {**dnames, **mnames})
+        run("p4q3c1a3b2p5q4c2b3d1q5e0h0c3g0h1d2g1h2e1h3g2d3h4g3e2h5e3", {**dnames, **mnames})
 
         @pl.loop(6, NOS)
         def _(i):
@@ -686,9 +690,9 @@
 
     @pl.when(end)
     def _():
-        run("c1a3b2d0c2b3d1e0c3g0d2g1e1g2d3e2e3", dnames)
-
-    run("g3g4", dnames)
+        run("c1a3b2b3c2d1e0c3g0d2d3e1g1e2g2e3g3", dnames)
+
+    run("g4", dnames)
     ev_ls()
     run("g5", dnames)
 
@@ -750,7 +754,7 @@
         (V, D), (T, D), (1, D), (8, 128), (4, V, PT), (3, T, D), (RA, D), (RA, D), (4, 4 * SG, D), (4, 2, SG, D), (4, 2, SG // 2, D))]
     bufs = [((T, D), BF16), ((T, D), BF16), ((RA + OW, D), F32), ((4, PV, PT), F32), ((3, PV, D), BF16), ((2, PT, D), F32), ((2, PT // 2, D), F32),
             ((max(z_.AG, SG), D), F32), ((SG // 2, D), BF16), ((2, 2, SG // 2, D), F32)]
-    row = ((8, T),) * 3 + ((2, 8, T),) + tuple((int(k), 1, T) for k in "42233") + ((4, 2, T), (3, 2, T))
+    row = ((8, T),) * 3 + ((1, T),) * 2 + ((2, 8, T),) + tuple((int(k), 1, T) for k in "42233") + ((4, 2, T), (3, 2, T))
     tiles = ((2, 8, 128),) * 4 + ((6, 8, D), (5, 8, D))
     bufs += [(s, F32) for s in row + tiles]
     pairs = ((z_.NAS,),) * 6 + ((z_.NOS,),) * 6
@@ -772,10 +776,8 @@
 def make(mesh, z_):
     def local_step(hidden, labels, loss_mask, norm_gain, w_shard):
         h = hidden.reshape(z_.T, z_.D)
-        lab = labels.reshape(1, z_.T).astype(F32)
-        msk = loss_mask.reshape(1, z_.T).astype(F32)
         gain = norm_gain.astype(F32).reshape(1, z_.D)
-        o = _call(z_, h, lab, msk, gain, w_shard.T)
+        o = _call(z_, h, labels, loss_mask, gain, w_shard.T)
         dw, dh, dg, loss = o[:4]
         return loss[0, 0], dh.astype(BF16).reshape(hidden.shape), dg.reshape(z_.D), dw.T
 

time: 574 us -> 567 us (0.988)
    unnamed x6 -> x4, local copies, waits for them, and re-layouts: 19.9 us -> 18.7 us
where the time goes in v3:
time: 567 us; the launch traced here: 564 us
  Pallas kernels  533 us (94%)
  local copies, waits for them, and re-layouts  19.8 us (3%)
  other arithmetic  10.4 us (2%)
    pallas_call x1, Pallas kernels, _call(): pl.pallas_call(functools.partial(_kernel, z_), out_shape=outs, in_specs=[...  533 us
    unnamed x4, local copies, waits for them, and re-layouts  18.7 us

profile of v3, /device:TPU:0, one launch (start us, length us, event | category | flops | bytes accessed | tf_op | source)
XLA Modules:
  0.0 564.2 jit_solution(6511845043963389536)
XLA Ops:
  0.6 1.3 reshape.27
  1.9 533.4 %lm_head.1 = (f32[6288,1024]{1,0:T(8,128)}, f32[4096,1024]{1,0:T(8,128)}, f32[1,1024]{1,0:T(1,128)}, f32[8,128]{1,0:T(8,128)}, f32[4,6288,1024]{2,1,0:T(8,128)},...) custom-call(bf16[4096,1024]{1,0:T(8,128)(2,1)} %bitcast.10, ...), custom_call_target="tpu_custom_call" | custom-call | tf_op jit(solution)/shard_map/lm_head/pallas_call | solution.py:765
  535.3 1.2 slice.3
  536.5 0.0 copy-start
  536.5 9.1 %convert_element_type.4 = bf16[4096,1024]{1,0:T(8,128)(2,1)} convert(f32[4096,1024]{1,0:T(8,128)} %get-tuple-element.9) | non-fusion elementwise | flops 4194304 | bytes 25165824 | tf_op jit(solution)/shard_map/convert_element_type | solution.py:782
  545.5 0.0 copy-done
  545.5 0.6 copy.11
  546.1 18.1 %copy.12 = f32[1024,6288]{0,1:T(8,128)} copy(f32[1024,6288]{0,1:T(8,128)} %bitcast.7) | data formatting | bytes 51511296
Async XLA Ops:
  536.5 9.1 %copy-start = (f32[1,1024]{1,0:T(1,128)S(1)}, f32[1,1024]{1,0:T(1,128)}, u32[]{:S(2)}) copy-start(f32[1,1024]{1,0:T(1,128)} %get-tuple-element.10) | copy-start | bytes 12292
